TPU v7x, 32 devices: a whole 2x2x4 slice. The times are simulated.
32 devices in a mesh: gx: 8 (over y, x, core), gy: 4 (over z).
Axes of the slice: x: 2, y: 2, z: 4, core: 2. Of those that a mesh axis runs over, the one named last changes fastest.
Arguments:
- east_class: int32 [512, 256], P('gx', 'gy'), may hold values from 0 to 7
- south_class: int32 [512, 256], P('gx', 'gy'), may hold values from 0 to 7
- cond_table: float32 [8], replicated, may hold values from 0.5 to 4
- leakage: float32 [512, 256], P('gx', 'gy'), may hold values from 0.1 to 1
- pad_mask: int32 [512, 256], P('gx', 'gy'), may hold values 0 or 1
- load_current: float32 [512, 256, 256], P('gx', 'gy'), may hold values from -24 to 24
Outputs:
- potential: float32 [512, 256, 256], P('gx', 'gy')
All inputs are finite; a program needn't handle non-finite values. No bound on the sum of `pad_mask` on one device may be relied on, other than what follows from the above.
Results may differ from a plain program's by a relative error of at most 0.00002.
Values sent between devices are 32-bit elements; how exact they have to be, the bound alone decides.
A program may use at most 64 MiB of HBM per device.

v0:
```python
import jax
import jax.numpy as jnp
from jax import lax
from jax.sharding import PartitionSpec as P

ITERS = 4


PAD_GAIN = 8.0
SPECTRAL_BOUND = 0.995


def with_halo(cells, sides, width):
    for axis, dim in sides:
        count = lax.axis_size(axis)
        head = lax.slice_in_dim(cells, 0, width, axis=dim)
        tail = lax.slice_in_dim(cells, cells.shape[dim] - width, cells.shape[dim], axis=dim)
        cells = jnp.concatenate(
            [
                lax.ppermute(tail, axis, [(i, (i + 1) % count) for i in range(count)]),
                cells,
                lax.ppermute(head, axis, [((i + 1) % count, i) for i in range(count)]),
            ],
            axis=dim,
        )
    return cells


def chebyshev_weights(total_steps):
    weights = [1.0]
    for position in range(1, total_steps):
        if position == 1:
            weights.append(1.0 / (1.0 - SPECTRAL_BOUND * SPECTRAL_BOUND / 2.0))
        else:
            weights.append(1.0 / (1.0 - SPECTRAL_BOUND * SPECTRAL_BOUND * weights[-1] / 4.0))
    return weights


def lookup(classes, cond_table):
    labels = jnp.arange(cond_table.shape[0], dtype=jnp.int32)
    matches = classes[:, :, None] == labels
    return jnp.sum(jnp.where(matches, cond_table, 0.0), axis=-1)


def trimmed(array, amount):
    return array[amount : array.shape[0] - amount, amount : array.shape[1] - amount]


def jacobi(padded_field, east_cond, south_cond, diagonal, source):
    neighbours = (
        east_cond[1:-1, 1:-1, None] * padded_field[1:-1, 2:]
        + east_cond[1:-1, :-2, None] * padded_field[1:-1, :-2]
    )
    neighbours = neighbours + south_cond[1:-1, 1:-1, None] * padded_field[2:, 1:-1]
    neighbours = neighbours + south_cond[:-2, 1:-1, None] * padded_field[:-2, 1:-1]
    return source + neighbours / diagonal[:, :, None]


def body(east_class, south_class, cond_table, leakage, pad_mask, load_current):
    east_cond = lookup(east_class, cond_table)
    south_cond = lookup(south_class, cond_table)
    pads = pad_mask.astype(jnp.float32)
    extra_diag = leakage + PAD_GAIN * pads
    omegas = chebyshev_weights(ITERS)
    stacked = jnp.stack([east_cond, south_cond, extra_diag, pads])
    widened = with_halo(stacked, (("gx", 1), ("gy", 2)), ITERS + 1)
    east_wide = widened[0]
    south_wide = widened[1]
    extra_wide = widened[2]
    cycle_diag = (
        east_wide[1:-1, 1:-1]
        + east_wide[1:-1, :-2]
        + south_wide[1:-1, 1:-1]
        + south_wide[:-2, 1:-1]
        + extra_wide[1:-1, 1:-1]
    )
    pads_cycle = widened[3][1:-1, 1:-1]
    load_wide = with_halo(load_current, (("gx", 0), ("gy", 1)), ITERS)
    source_all = (PAD_GAIN * pads_cycle[:, :, None] - load_wide) / cycle_diag[:, :, None]
    field = source_all
    previous = source_all
    for iteration in range(ITERS):
        cut = iteration + 1
        jacobi_value = jacobi(
            field,
            trimmed(east_wide, cut),
            trimmed(south_wide, cut),
            trimmed(cycle_diag, cut),
            trimmed(source_all, cut),
        )
        if iteration == 0:
            updated = jacobi_value
        else:
            older = trimmed(previous, 2)
            updated = omegas[iteration] * (jacobi_value - older) + older
        previous, field = (field, updated)
    return field


def solution(mesh):
    in_specs = (
        P("gx", "gy"),
        P("gx", "gy"),
        P(),
        P("gx", "gy"),
        P("gx", "gy"),
        P("gx", "gy", None),
    )
    out_specs = P("gx", "gy", None)
    return jax.shard_map(body, mesh=mesh, in_specs=in_specs, out_specs=out_specs, check_vma=False)
```

profile of v0, /device:TPU:0, one launch (start us, length us, event | category | flops | bytes accessed | tf_op | source)
XLA Modules:
  0.0 71.4 jit_solution(13719251896380119397)
XLA Ops:
  0.0 0.8 %convert_bitcast_fusion = f32[1,64,64]{2,1,0:T(8,128)S(1)} fusion(s32[64,64]{1,0:T(8,128)} %param.10), kind=kLoop, calls=%fused_computation.65 | loop fusion | flops 4096 | bytes 32768 | tf_op jit(solution)/shard_map/stack | solution.py:65
  0.8 0.8 %add_bitcast_fusion = f32[1,64,64]{2,1,0:T(8,128)S(1)} fusion(f32[64,64]{1,0:T(8,128)} %param.9, s32[64,64]{1,0:T(8,128)} %param.10), kind=kLoop, calls=%fused_computation.64 | loop fusion | flops 12288 | bytes 49152 | tf_op jit(solution)/shard_map/stack | solution.py:65
  1.5 1.0 %select_reduce_fusion.1 = (f32[64,64]{1,0:T(8,128)S(1)}, f32[64,64]{1,0:T(8,128)S(1)}) fusion(f32[8]{0:T(128)} %param.8, s32[64,64]{1,0:T(8,128)} %param.6, s32[64,64]{1,0:T(8,128)} %param.7), kind=kLoop, calls=%fused_computation.51 | loop fusion | flops 188416 | bytes 65568 | tf_op jit(solution)/shard_map/reduce_sum | solution.py:42
  2.6 0.5 collective-permute-start
  3.1 2.9 %collective-permute-start.1 = (f32[4,5,64]{2,1,0:T(8,128)S(1)}, f32[4,5,64]{2,1,0:T(8,128)S(1)}, u32[]{:S(2)}, u32[]{:S(2)}) collective-permute-start(f32[4,5,64]{2,1,0:T(8,128)S(1)} %get-tuple-element.18), channel_id=1, source_target_pairs={{4,0},{8,4},{12,8},{16,12},{20,16},{24,20},{28,24},{0,28},{5,1},{9... | collective-permute-start | bytes 15368 | tf_op jit(solution)/shard_map/ppermute | solution.py:22
  6.1 4.6 %copy.34 = f32[64,64,256]{2,0,1:T(8,128)S(1)} copy(f32[64,64,256]{2,1,0:T(8,128)} %param.11) | data formatting | bytes 8388608 | tf_op args[5]
  10.7 0.0 copy-start
  10.7 0.0 collective-permute-done
  10.7 0.0 collective-permute-done.1
  10.8 0.1 fusion.29
  10.9 2.3 %collective-permute-start.2 = (f32[4,74,5]{2,1,0:T(8,128)S(1)}, f32[4,74,5]{2,1,0:T(8,128)S(1)}, u32[]{:S(2)}, u32[]{:S(2)}) collective-permute-start(f32[4,74,5]{2,1,0:T(8,128)S(1)} %get-tuple-element.15), channel_id=1, source_target_pairs={{0,1},{1,2},{2,3},{3,0},{4,5},{5,6},{6,7},{7,4},{8,9},{9,10},{10,1... | collective-permute-start | bytes 17768 | tf_op jit(solution)/shard_map/ppermute | solution.py:20
  13.2 2.1 %collective-permute-start.3 = (f32[4,74,5]{2,1,0:T(8,128)S(1)}, f32[4,74,5]{2,1,0:T(8,128)S(1)}, u32[]{:S(2)}, u32[]{:S(2)}) collective-permute-start(f32[4,74,5]{2,1,0:T(8,128)S(1)} %get-tuple-element.16), channel_id=1, source_target_pairs={{1,0},{2,1},{3,2},{0,3},{5,4},{6,5},{7,6},{4,7},{9,8},{10,9},{11,1... | collective-permute-start | bytes 17768 | tf_op jit(solution)/shard_map/ppermute | solution.py:22
  15.3 0.1 fusion.28
  15.4 0.1 collective-permute-start.4
  15.4 2.6 %collective-permute-start.5 = (f32[4,64,256]{2,0,1:T(4,128)S(1)}, f32[4,64,256]{2,0,1:T(4,128)S(1)}, u32[]{:S(2)}, u32[]{:S(2)}) collective-permute-start(f32[4,64,256]{2,0,1:T(4,128)S(1)} %get-tuple-element.10), channel_id=1, source_target_pairs={{4,0},{8,4},{12,8},{16,12},{20,16},{24,20},{28,24},{0,28},{5,1},{9... | collective-permute-start | bytes 786440 | tf_op jit(solution)/shard_map/ppermute | solution.py:22
  18.1 2.2 %collective-permute-done.2 = f32[4,74,5]{2,1,0:T(8,128)S(1)} collective-permute-done((f32[4,74,5]{2,1,0:T(8,128)S(1)}, f32[4,74,5]{2,1,0:T(8,128)S(1)}, u32[]{:S(2)}, u32[]{:S(2)}) %collective-permute-start.2) | collective-permute-done | bytes 5952 | tf_op jit(solution)/shard_map/ppermute | solution.py:20
  20.3 1.2 %collective-permute-done.3 = f32[4,74,5]{2,1,0:T(8,128)S(1)} collective-permute-done((f32[4,74,5]{2,1,0:T(8,128)S(1)}, f32[4,74,5]{2,1,0:T(8,128)S(1)}, u32[]{:S(2)}, u32[]{:S(2)}) %collective-permute-start.3) | collective-permute-done | bytes 5952 | tf_op jit(solution)/shard_map/ppermute | solution.py:22
  21.5 0.2 pad_maximum_fusion.4
  21.7 0.1 fusion.36
  21.8 0.1 fusion.34
  21.9 0.1 fusion.32
  22.0 1.8 %collective-permute-done.4 = f32[4,64,256]{2,0,1:T(4,128)S(1)} collective-permute-done((f32[4,64,256]{2,0,1:T(4,128)S(1)}, f32[4,64,256]{2,0,1:T(4,128)S(1)}, u32[]{:S(2)}, u32[]{:S(2)}) %collective-permute-start.4) | collective-permute-done | bytes 262176 | tf_op jit(solution)/shard_map/ppermute | solution.py:20
  23.8 0.0 collective-permute-done.5
  23.8 0.0 copy-done
  23.8 0.1 pad_maximum_fusion.2
  23.9 0.1 collective-permute-start.6
  24.1 3.7 %collective-permute-start.7 = (f32[72,4,256]{2,0,1:T(8,128)S(1)}, f32[72,4,256]{2,0,1:T(8,128)S(1)}, u32[]{:S(2)}, u32[]{:S(2)}) collective-permute-start(f32[72,4,256]{2,0,1:T(8,128)S(1)} %get-tuple-element.8), channel_id=1, source_target_pairs={{1,0},{2,1},{3,2},{0,3},{5,4},{6,5},{7,6},{4,7},{9,8},{10,9},{11,1... | collective-permute-start | bytes 884744 | tf_op jit(solution)/shard_map/ppermute | solution.py:22
  27.8 0.1 slice_add_fusion
  27.9 0.1 copy.37
  28.0 0.1 slice.294
  28.1 0.1 slice.302
  28.2 0.1 slice.310
  28.2 0.1 slice.319
  28.3 0.1 copy.33
  28.4 0.1 copy.45
  28.5 0.1 copy.41
  28.6 0.1 copy.42
  28.7 0.1 copy.43
  28.8 0.1 copy.44
  28.9 0.1 copy.49
  29.0 0.1 copy.40
  29.1 0.1 copy.46
  29.2 0.1 copy.47
  29.3 0.1 copy.48
  29.4 0.1 copy.53
  29.5 0.1 copy.39
  29.6 0.1 copy.50
  29.7 0.1 copy.51
  29.8 0.1 copy.52
  29.9 0.1 copy.57
  30.0 0.1 fusion.30
  30.1 0.1 copy.38
  30.2 0.1 copy.54
  30.2 0.1 copy.55
  30.3 0.1 copy.56
  30.4 5.3 %collective-permute-done.6 = f32[72,4,256]{2,0,1:T(8,128)S(1)} collective-permute-done((f32[72,4,256]{2,0,1:T(8,128)S(1)}, f32[72,4,256]{2,0,1:T(8,128)S(1)}, u32[]{:S(2)}, u32[]{:S(2)}) %collective-permute-start.6) | collective-permute-done | bytes 294944 | tf_op jit(solution)/shard_map/ppermute | solution.py:20
  35.7 4.5 %collective-permute-done.7 = f32[72,4,256]{2,0,1:T(8,128)S(1)} collective-permute-done((f32[72,4,256]{2,0,1:T(8,128)S(1)}, f32[72,4,256]{2,0,1:T(8,128)S(1)}, u32[]{:S(2)}, u32[]{:S(2)}) %collective-permute-start.7) | collective-permute-done | bytes 294944 | tf_op jit(solution)/shard_map/ppermute | solution.py:22
  40.3 5.3 %fusion = f32[72,72,256]{2,0,1:T(8,128)S(1)} fusion(f32[72,4,256]{2,0,1:T(8,128)S(1)} %collective-permute-done.7, f32[4,64,256]{2,0,1:T(4,128)S(1)} %collective-permute-done.5, f32[64,64,256]{2,0,1:T(8,128)} %copy-done, f32[4,64,256]{2,0,1:T(4,128)S(1)} %collective-permute-done.4, f32[72,4,256]{2,0,1:T(8,128)S(1)} %collective-permute-done.6, ...), kind=kLoop, calls=%fused_computation.2 | loop fusion | flops 7962624 | bytes 10658304 | tf_op jit(solution)/shard_map/div | solution.py:79
  45.6 4.5 %fusion.3 = f32[70,70,256]{2,0,1:T(8,128)S(1)} fusion(f32[72,72,256]{2,0,1:T(8,128)S(1)} %fusion, f32[70,70]{0,1:T(8,128)S(1)} %copy.45, f32[70,70]{0,1:T(8,128)S(1)} %copy.44, f32[70,70]{0,1:T(8,128)S(1)} %copy.43, f32[70,70]{0,1:T(8,128)S(1)} %copy.42, f32[70,70]{0,1:T(8,128)S(1)} %copy.41), kind=kLoop, calls=%fused_computation.6 | loop fusion | flops 11289600 | bytes 30203600 | tf_op jit(solution)/shard_map/add | solution.py:56
  50.1 5.0 %fusion.7 = f32[68,68,256]{2,0,1:T(8,128)S(1)} fusion(f32[70,70,256]{2,0,1:T(8,128)S(1)} %fusion.3, f32[72,72,256]{2,0,1:T(8,128)S(1)} %fusion, f32[68,68]{0,1:T(8,128)S(1)} %copy.49, f32[68,68]{0,1:T(8,128)S(1)} %copy.48, f32[68,68]{0,1:T(8,128)S(1)} %copy.47, f32[68,68]{0,1:T(8,128)S(1)} %copy.46, f32[68,68]{0,1:T(8,128)S(1)} %copy.40), kind=kLoop, calls=%fused_computation.13 | loop fusion | flops 14204928 | bytes 28502336 | tf_op jit(solution)/shard_map/add | solution.py:95
  55.1 6.4 %fusion.17 = f32[66,66,256]{2,0,1:T(8,128)S(1)} fusion(f32[68,68,256]{2,0,1:T(8,128)S(1)} %fusion.7, f32[70,70,256]{2,0,1:T(8,128)S(1)} %fusion.3, f32[72,72,256]{2,0,1:T(8,128)S(1)} %fusion, f32[66,66]{0,1:T(8,128)S(1)} %copy.53, f32[66,66]{0,1:T(8,128)S(1)} %copy.52, f32[66,66]{0,1:T(8,128)S(1)} %copy.51, f32[66,66]{0,1:T(8,128)S(1)} %copy.50, ...), kind=kLoop, calls=%fused_computation.28 | loop fusion | flops 13381632 | bytes 31310928 | tf_op jit(solution)/shard_map/add | solution.py:95
  61.6 5.4 %fusion.25 = f32[64,64,256]{2,0,1:T(8,128)S(1)} fusion(f32[66,66,256]{2,0,1:T(8,128)S(1)} %fusion.17, f32[68,68,256]{2,0,1:T(8,128)S(1)} %fusion.7, f32[72,72,256]{2,0,1:T(8,128)S(1)} %fusion, f32[64,64]{0,1:T(8,128)S(1)} %copy.57, f32[64,64]{0,1:T(8,128)S(1)} %copy.56, f32[64,64]{0,1:T(8,128)S(1)} %copy.55, f32[64,64]{0,1:T(8,128)S(1)} %copy.54, ...), kind=kLoop, calls=%fused_computation.40 | loop fusion | flops 12582912 | bytes 29442048 | tf_op jit(solution)/shard_map/add | solution.py:95
  67.0 4.4 %copy.58 = f32[64,64,256]{2,1,0:T(8,128)} copy(f32[64,64,256]{2,0,1:T(8,128)S(1)} %fusion.25) | data formatting | bytes 8388608 | tf_op jit(solution)/shard_map/add | solution.py:95
  (3 shorter events, 0.0 us)
Async XLA Ops:
  2.6 8.1 %collective-permute-start = (f32[4,5,64]{2,1,0:T(8,128)S(1)}, f32[4,5,64]{2,1,0:T(8,128)S(1)}, u32[]{:S(2)}, u32[]{:S(2)}) collective-permute-start(f32[4,5,64]{2,1,0:T(8,128)S(1)} %get-tuple-element.17), channel_id=1, source_target_pairs={{0,4},{4,8},{8,12},{12,16},{16,20},{20,24},{24,28},{28,0},{1,5},{5... | collective-permute-start | bytes 15368 | tf_op jit(solution)/shard_map/ppermute | solution.py:20
  3.1 7.6 %collective-permute-start.1 = (f32[4,5,64]{2,1,0:T(8,128)S(1)}, f32[4,5,64]{2,1,0:T(8,128)S(1)}, u32[]{:S(2)}, u32[]{:S(2)}) collective-permute-start(f32[4,5,64]{2,1,0:T(8,128)S(1)} %get-tuple-element.18), channel_id=1, source_target_pairs={{4,0},{8,4},{12,8},{16,12},{20,16},{24,20},{28,24},{0,28},{5,1},{9... | collective-permute-start | bytes 15368 | tf_op jit(solution)/shard_map/ppermute | solution.py:22
  10.7 13.1 %copy-start = (f32[64,64,256]{2,0,1:T(8,128)}, f32[64,64,256]{2,0,1:T(8,128)S(1)}, u32[]{:S(2)}) copy-start(f32[64,64,256]{2,0,1:T(8,128)S(1)} %copy.34) | copy-start | bytes 12582916
  10.9 9.4 %collective-permute-start.2 = (f32[4,74,5]{2,1,0:T(8,128)S(1)}, f32[4,74,5]{2,1,0:T(8,128)S(1)}, u32[]{:S(2)}, u32[]{:S(2)}) collective-permute-start(f32[4,74,5]{2,1,0:T(8,128)S(1)} %get-tuple-element.15), channel_id=1, source_target_pairs={{0,1},{1,2},{2,3},{3,0},{4,5},{5,6},{6,7},{7,4},{8,9},{9,10},{10,1... | collective-permute-start | bytes 17768 | tf_op jit(solution)/shard_map/ppermute | solution.py:20
  13.2 8.3 %collective-permute-start.3 = (f32[4,74,5]{2,1,0:T(8,128)S(1)}, f32[4,74,5]{2,1,0:T(8,128)S(1)}, u32[]{:S(2)}, u32[]{:S(2)}) collective-permute-start(f32[4,74,5]{2,1,0:T(8,128)S(1)} %get-tuple-element.16), channel_id=1, source_target_pairs={{1,0},{2,1},{3,2},{0,3},{5,4},{6,5},{7,6},{4,7},{9,8},{10,9},{11,1... | collective-permute-start | bytes 17768 | tf_op jit(solution)/shard_map/ppermute | solution.py:22
  15.4 8.5 %collective-permute-start.4 = (f32[4,64,256]{2,0,1:T(4,128)S(1)}, f32[4,64,256]{2,0,1:T(4,128)S(1)}, u32[]{:S(2)}, u32[]{:S(2)}) collective-permute-start(f32[4,64,256]{2,0,1:T(4,128)S(1)} %get-tuple-element.9), channel_id=1, source_target_pairs={{0,4},{4,8},{8,12},{12,16},{16,20},{20,24},{24,28},{28,0},{1,5},{5... | collective-permute-start | bytes 786440 | tf_op jit(solution)/shard_map/ppermute | solution.py:20
  15.4 8.4 %collective-permute-start.5 = (f32[4,64,256]{2,0,1:T(4,128)S(1)}, f32[4,64,256]{2,0,1:T(4,128)S(1)}, u32[]{:S(2)}, u32[]{:S(2)}) collective-permute-start(f32[4,64,256]{2,0,1:T(4,128)S(1)} %get-tuple-element.10), channel_id=1, source_target_pairs={{4,0},{8,4},{12,8},{16,12},{20,16},{24,20},{28,24},{0,28},{5,1},{9... | collective-permute-start | bytes 786440 | tf_op jit(solution)/shard_map/ppermute | solution.py:22
  23.9 11.8 %collective-permute-start.6 = (f32[72,4,256]{2,0,1:T(8,128)S(1)}, f32[72,4,256]{2,0,1:T(8,128)S(1)}, u32[]{:S(2)}, u32[]{:S(2)}) collective-permute-start(f32[72,4,256]{2,0,1:T(8,128)S(1)} %get-tuple-element.7), channel_id=1, source_target_pairs={{0,1},{1,2},{2,3},{3,0},{4,5},{5,6},{6,7},{7,4},{8,9},{9,10},{10,1... | collective-permute-start | bytes 884744 | tf_op jit(solution)/shard_map/ppermute | solution.py:20
  24.1 16.2 %collective-permute-start.7 = (f32[72,4,256]{2,0,1:T(8,128)S(1)}, f32[72,4,256]{2,0,1:T(8,128)S(1)}, u32[]{:S(2)}, u32[]{:S(2)}) collective-permute-start(f32[72,4,256]{2,0,1:T(8,128)S(1)} %get-tuple-element.8), channel_id=1, source_target_pairs={{1,0},{2,1},{3,2},{0,3},{5,4},{6,5},{7,6},{4,7},{9,8},{10,9},{11,1... | collective-permute-start | bytes 884744 | tf_op jit(solution)/shard_map/ppermute | solution.py:22
where the time goes:
time: 71.9 us; the launch traced here: 71.4 us
  other arithmetic  29.7 us (41%)
  waiting for transfers between devices  15.1 us (21%)
  starting transfers between devices  14.5 us (20%)
  local copies, waits for them, and re-layouts  12 us (17%)
    add x3, other arithmetic, body(): updated = omegas[iteration] * (jacobi_value - older) + older  16.9 us
    ppermute x4, starting transfers between devices, with_halo(): lax.ppermute(head, axis, [((i + 1) % count, i) for i in range(count)])  11.4 us
    ppermute x4, waiting for transfers between devices, with_halo(): lax.ppermute(tail, axis, [(i, (i + 1) % count) for i in range(count)])  9.33 us
    ppermute x4, waiting for transfers between devices, with_halo(): lax.ppermute(head, axis, [((i + 1) % count, i) for i in range(count)])  5.75 us
    div x1, other arithmetic, body(): (PAD_GAIN * pads_cycle[:, :, None] - load_wide) / cycle_diag[:, :, None]  5.34 us
    unnamed x3, local copies, waits for them, and re-layouts  4.62 us
    add x1, other arithmetic, jacobi(): return source + neighbours / diagonal[:, :, None]  4.52 us
    add x1, local copies, waits for them, and re-layouts, body(): updated = omegas[iteration] * (jacobi_value - older) + older  4.44 us
  transfers between devices with their start and end apart: 8, of which 5 were waited for; matrix products, arithmetic and copies ran while one was open for 11% of the time, Pallas kernels for 0%

commit v1 on v0

v1 whole, which is shorter than its diff:
```python
import functools

import jax
import jax.numpy as jnp
from jax import lax
from jax.experimental import pallas as pl
from jax.experimental.pallas import tpu as pltpu
from jax.sharding import PartitionSpec as P

ITERS = 4
PAD_GAIN = 8.0
SPECTRAL_BOUND = 0.995
G = ITERS
MESH = pl.DeviceIdType.MESH
CHUNKS = 2


def polynomial():
    weights = [1.0]
    for k in range(1, ITERS):
        if k == 1:
            weights.append(1.0 / (1.0 - SPECTRAL_BOUND**2 / 2.0))
        else:
            weights.append(1.0 / (1.0 - SPECTRAL_BOUND**2 * weights[-1] / 4.0))
    size = ITERS + 1
    previous = [1.0] + [0.0] * (size - 1)
    field = [1.0, 1.0] + [0.0] * (size - 2)
    for k in range(1, ITERS):
        jac = [1.0] + field[:-1]
        updated = [weights[k] * (a - b) + b for a, b in zip(jac, previous)]
        previous, field = field, updated
    return field


def kernel(
    nx, ny, rows, cols,
    table_ref, east_ref, south_ref, leak_ref, pad_ref, x_ref, o_ref,
    cf, tw, ew_src, ew_dst, load, src, v1, v2, v3, bc,
    eload, esrc, e1, e2, e3, ebc,
    local_sem, send_sem, recv_sem,
):
    mx, my = lax.axis_index("gx"), lax.axis_index("gy")
    north, south = lax.rem(mx + nx - 1, nx), lax.rem(mx + 1, nx)
    west, east = lax.rem(my + ny - 1, ny), lax.rem(my + 1, ny)
    cases = x_ref.shape[2]
    halves = [slice(h * 128, (h + 1) * 128) for h in range(cases // 128)]
    poly = polynomial()

    barrier = pltpu.get_barrier_semaphore()
    peers = [
        (north, my), (south, my), (mx, west), (mx, east),
        (north, west), (north, east), (south, west), (south, east),
    ]
    for peer in peers:
        pl.semaphore_signal(barrier, inc=1, device_id=peer, device_id_type=MESH)
    own = pltpu.make_async_copy(x_ref, load.at[pl.ds(G, rows)], local_sem)
    own.start()

    def lookup(classes):
        value = jnp.full(classes.shape, table_ref[0], jnp.float32)
        for c in range(1, table_ref.shape[0]):
            value = jnp.where(classes == c, table_ref[c], value)
        return value

    blank = jnp.zeros((rows, 128 - cols), jnp.float32)
    fields = [
        lookup(east_ref[...]),
        lookup(south_ref[...]),
        leak_ref[...] + PAD_GAIN * pad_ref[...].astype(jnp.float32),
    ]
    for f in range(3):
        cf[f, pl.ds(8, rows), :] = jnp.concatenate([fields[f], blank], axis=1)
    square = jnp.concatenate([fields[0], blank], axis=1)
    above, below = jnp.zeros((8, 128), jnp.float32), jnp.zeros((120 - rows, 128), jnp.float32)
    square = jnp.concatenate([above, square, below], axis=0)
    ew_src[...] = jnp.transpose(square)[cols - 8 : cols, :]

    pl.semaphore_wait(barrier, len(peers))

    counter = [0]

    def send(source, target, device):
        n = counter[0]
        counter[0] += 1
        copy = pltpu.make_async_remote_copy(
            src_ref=source, dst_ref=target,
            send_sem=send_sem.at[n], recv_sem=recv_sem.at[n],
            device_id=device, device_id_type=MESH,
        )
        copy.start()
        return copy

    cf_n = send(cf.at[:, pl.ds(rows, 8)], cf.at[:, pl.ds(0, 8)], (south, my))
    cf_s = send(cf.at[:, pl.ds(8, 8)], cf.at[:, pl.ds(rows + 8, 8)], (north, my))
    ew = send(ew_src, ew_dst, (mx, east))
    ld_n = send(x_ref.at[pl.ds(rows - G, G)], load.at[pl.ds(0, G)], (south, my))
    ld_s = send(x_ref.at[pl.ds(0, G)], load.at[pl.ds(rows + G, G)], (north, my))
    half = rows // CHUNKS
    low, high = pl.ds(0, G), pl.ds(cols - G, G)
    to_left, to_right = pl.ds(0, G), pl.ds(G, G)
    D = G - 1

    def side(start, count, at, row_from, vertical):
        return [
            send(
                x_ref.at[pl.ds(row_from, count), high],
                eload.at[0, pl.ds(at, count), to_left],
                (vertical, east),
            ),
            send(
                x_ref.at[pl.ds(row_from, count), low],
                eload.at[1, pl.ds(at, count), to_right],
                (vertical, west),
            ),
        ]

    first = side(0, half, G, 0, mx)
    first += side(0, D, G - D, rows - D, south)

    cf_n.wait_recv()
    cf_s.wait_recv()
    for f in range(3):
        tw[f, pl.ds(8, cols), :] = jnp.transpose(cf[f])[0:cols, :]
    tw_w = send(tw.at[:, pl.ds(cols, 8)], tw.at[:, pl.ds(0, 8)], (mx, east))
    tw_e = send(tw.at[:, pl.ds(8, 8)], tw.at[:, pl.ds(cols + 8, 8)], (mx, west))
    second = side(0, rows - half, G + half, half, mx)
    second += side(0, D, rows + G, 0, north)

    def coefficients(e, e_west, s, extra):
        s_north = pltpu.roll(s, 1, 1)
        rd = 1.0 / (e + e_west + s + s_north + extra)
        pads = jnp.where(extra > PAD_GAIN / 2, PAD_GAIN, 0.0)
        return [e * rd, e_west * rd, s * rd, s_north * rd, rd, pads * rd]

    def spread(values, put, lo, count):
        def one(r):
            for q, value in enumerate(values):
                lane = pltpu.roll(value, lax.rem(128 - (r + 8 - G), 128), 1)
                put(q, r, jnp.broadcast_to(lane[:, 0:1], value.shape))
        lax.fori_loop(lo, lo + count, lambda r, c: (one(r), c)[1], 0)

    def put_own(q, r, value):
        bc[q, r] = value

    ew.wait_recv()
    e_own = tw[0, pl.ds(8, cols), :]
    column = lax.broadcasted_iota(jnp.int32, (cols, 128), 0)
    e_first = jnp.broadcast_to(ew_dst[7:8, :], (cols, 128))
    e_west = jnp.where(column == 0, e_first, pltpu.roll(e_own, 1, 0))
    spread(
        coefficients(e_own, e_west, tw[1, pl.ds(8, cols), :], tw[2, pl.ds(8, cols), :]),
        put_own, G, rows,
    )

    def source(lo, count):
        def one(r, c):
            for h in halves:
                src[r, :, h] = bc[5, r] - load[r, :, h] * bc[4, r]
            return c
        lax.fori_loop(lo, lo + count, one, 0)

    chain = [src, v1, v2, v3]
    echain = [esrc, e1, e2, e3]

    def store(k, r, h, value):
        if k == ITERS:
            o_ref[r - G, :, h] = value
        else:
            chain[k][r, :, h] = value

    def step(k, lo, count):
        vin = chain[k - 1]

        def one(r, c):
            for h in halves:
                row = vin[r, :, h]
                total = bc[0, r] * pltpu.roll(row, cols - 1, 0)
                total += bc[1, r] * pltpu.roll(row, 1, 0)
                total += bc[2, r] * vin[r + 1, :, h]
                total += bc[3, r] * vin[r - 1, :, h]
                if k == 1:
                    total = total * poly[ITERS]
                store(k, r, h, total + poly[ITERS - k] * src[r, :, h])
            return c

        lax.fori_loop(lo, lo + count, one, 0)

    own.wait()
    source(G, rows)
    for k in range(1, ITERS + 1):
        step(k, G + k, rows - 2 * k)

    tw_w.wait_recv()
    tw_e.wait_recv()

    def wide(start, size):
        area = pl.ds(start, size)
        return coefficients(
            tw[0, area, :], tw[0, pl.ds(start - 1, size), :], tw[1, area, :], tw[2, area, :]
        )

    k_own = wide(8, cols)
    spread(k_own, put_own, 0, G)
    spread(k_own, put_own, rows + G, G)
    k_left, k_right = wide(8 - G, 2 * G), wide(8 + cols - G, 2 * G)

    def put_edge(w, q, r, value):
        ebc[w, q, r] = value

    spread(k_left, functools.partial(put_edge, 0), 0, rows + 2 * G)
    spread(k_right, functools.partial(put_edge, 1), 0, rows + 2 * G)
    ld_n.wait_recv()
    ld_s.wait_recv()
    source(0, G)
    source(rows + G, G)
    for k in range(1, ITERS + 1):
        step(k, k, G)
        step(k, rows + 2 * G - k - G, G)

    lane_row = lax.broadcasted_iota(jnp.int32, (2 * G, 128), 0)
    tiles = [pl.ds(0, 2 * G), pl.ds(cols - 2 * G, 2 * G)]

    def edge_source(lo, count):
        def one(r, c):
            for h in halves:
                for w in range(2):
                    ghost = ebc[w, 5, r] - eload[w, r, :, h] * ebc[w, 4, r]
                    mine = pltpu.roll(src[r, tiles[w], h], G, 0)
                    keep = lane_row < G if w == 0 else lane_row >= G
                    esrc[w, r, :, h] = jnp.where(keep, ghost, mine)
            return c
        lax.fori_loop(lo, lo + count, one, 0)

    def edge_step(k, lo, count):
        vin, base = echain[k - 1], chain[k - 1]

        def one(r, c):
            for h in halves:
                for w in range(2):
                    row = vin[w, r, :, h]
                    inner = base[r, tiles[w], h]
                    to_east, to_west = pltpu.roll(row, 2 * G - 1, 0), pltpu.roll(row, 1, 0)
                    if w == 0:
                        to_east = jnp.where(lane_row == 2 * G - 1, pltpu.roll(inner, G - 1, 0), to_east)
                    else:
                        to_west = jnp.where(lane_row == 0, pltpu.roll(inner, G + 1, 0), to_west)
                    total = ebc[w, 0, r] * to_east + ebc[w, 1, r] * to_west
                    total += ebc[w, 2, r] * vin[w, r + 1, :, h]
                    total += ebc[w, 3, r] * vin[w, r - 1, :, h]
                    if k == 1:
                        total = total * poly[ITERS]
                    total += poly[ITERS - k] * esrc[w, r, :, h]
                    if k < ITERS:
                        echain[k][w, r, :, h] = total
                    else:
                        keep = lane_row < G if w == 0 else lane_row >= G
                        mixed = jnp.where(keep, pltpu.roll(total, G, 0), o_ref[r - G, tiles[w], h])
                        o_ref[r - G, tiles[w], h] = mixed
            return c

        lax.fori_loop(lo, lo + count, one, 0)

    for copy in first:
        copy.wait_recv()
    cut = G + half
    edge_source(0, cut)
    for k in range(1, ITERS + 1):
        edge_step(k, k, cut - 2 * k)
    for copy in second:
        copy.wait_recv()
    edge_source(cut, rows + 2 * G - cut)
    for k in range(1, ITERS + 1):
        edge_step(k, cut - k, rows + 2 * G - cut)
    for copy in [cf_n, cf_s, ew, ld_n, ld_s, tw_w, tw_e] + first + second:
        copy.wait_send()


def body(nx, ny, east_class, south_class, cond_table, leakage, pad_mask, load_current):
    rows, cols, cases = load_current.shape
    tall = rows + 2 * G
    f32 = jnp.float32
    vmem = pl.BlockSpec(memory_space=pltpu.VMEM)
    copies = 7 + 8
    return pl.pallas_call(
        functools.partial(kernel, nx, ny, rows, cols),
        out_shape=jax.ShapeDtypeStruct(load_current.shape, f32),
        in_specs=[pl.BlockSpec(memory_space=pltpu.SMEM), vmem, vmem, vmem, vmem,
                  pl.BlockSpec(memory_space=pl.ANY)],
        out_specs=vmem,
        scratch_shapes=[
            pltpu.VMEM((3, 128, 128), f32),
            pltpu.VMEM((3, cols + 16, 128), f32),
            pltpu.VMEM((8, 128), f32),
            pltpu.VMEM((8, 128), f32),
            pltpu.VMEM((tall, cols, cases), f32),
            pltpu.VMEM((tall, cols, cases), f32),
            pltpu.VMEM((tall, cols, cases), f32),
            pltpu.VMEM((tall, cols, cases), f32),
            pltpu.VMEM((tall, cols, cases), f32),
            pltpu.VMEM((6, tall, cols, 128), f32),
            pltpu.VMEM((2, tall, 2 * G, cases), f32),
            pltpu.VMEM((2, tall, 2 * G, cases), f32),
            pltpu.VMEM((2, tall, 2 * G, cases), f32),
            pltpu.VMEM((2, tall, 2 * G, cases), f32),
            pltpu.VMEM((2, tall, 2 * G, cases), f32),
            pltpu.VMEM((2, 6, tall, 2 * G, 128), f32),
            pltpu.SemaphoreType.DMA,
            pltpu.SemaphoreType.DMA((copies,)),
            pltpu.SemaphoreType.DMA((copies,)),
        ],
        compiler_params=pltpu.CompilerParams(
            collective_id=0, has_side_effects=True, vmem_limit_bytes=67043328,
        ),
    )(cond_table, east_class, south_class, leakage, pad_mask, load_current)


def solution(mesh):
    in_specs = (
        P("gx", "gy"),
        P("gx", "gy"),
        P(),
        P("gx", "gy"),
        P("gx", "gy"),
        P("gx", "gy", None),
    )
    out_specs = P("gx", "gy", None)
    call = functools.partial(body, mesh.shape["gx"], mesh.shape["gy"])
    return jax.shard_map(call, mesh=mesh, in_specs=in_specs, out_specs=out_specs, check_vma=False)
```

time: 71.9 us -> 68.8 us (0.957)
  Pallas kernels: 0 us -> 63.9 us
  other arithmetic: 29.7 us -> 0 us
  waiting for transfers between devices: 15.1 us -> 0 us
  starting transfers between devices: 14.5 us -> 0 us
  local copies, waits for them, and re-layouts: 12 us -> 4.7 us
    pallas_call x0 -> x1, Pallas kernels: none -> 63.9 us  [body(): pl.pallas_call(functools.partial(kernel, nx, ny, rows, cols), out_shape=j...]
    add x5 -> x0, other arithmetic: 21.5 us -> none  [the longest x3 16.9 us: body(): updated = omegas[iteration] * (jacobi_value - older) + older]
    ppermute x8 -> x0, waiting for transfers between devices: 15.1 us -> none  [the longest x4 9.33 us: with_halo(): lax.ppermute(tail, axis, [(i, (i + 1) % count) for i in range(count)])]
    ppermute x8 -> x0, starting transfers between devices: 14.5 us -> none  [the longest x4 11.4 us: with_halo(): lax.ppermute(head, axis, [((i + 1) % count, i) for i in range(count)])]
    div x1 -> x0, other arithmetic: 5.34 us -> none  [body(): (PAD_GAIN * pads_cycle[:, :, None] - load_wide) / cycle_diag[:, :, None]]
    add x2 -> x0, local copies, waits for them, and re-layouts: 4.52 us -> none  [the longest x1 4.44 us: body(): updated = omegas[iteration] * (jacobi_value - older) + older]
    slice x30 -> x0, local copies, waits for them, and re-layouts: 2.79 us -> none  [the longest x8 0.8 us: jacobi(): east_cond[1:-1, 1:-1, None] * padded_field[1:-1, 2:]]
    another operation x2 -> x0, other arithmetic: 1.54 us -> none  [body(): stacked = jnp.stack([east_cond, south_cond, extra_diag, pads])]
  transfers between devices with their start and end apart: 8 -> 0, of which waited for: 5 -> 0; matrix products, arithmetic and copies ran while one was open for 11% -> 0% of each run, Pallas kernels for 0% -> 0%
where the time goes in v1:
time: 68.8 us; the launch traced here: 68.6 us
  Pallas kernels  63.9 us (93%)
  local copies, waits for them, and re-layouts  4.7 us (7%)
    pallas_call x1, Pallas kernels, body(): pl.pallas_call(functools.partial(kernel, nx, ny, rows, cols), out_shape=j...  63.9 us
    unnamed x1, local copies, waits for them, and re-layouts  4.7 us

profile of v1, /device:TPU:0, one launch (start us, length us, event | category | flops | bytes accessed | tf_op | source)
XLA Modules:
  0.0 68.6 jit_solution(9452661449179257509)
XLA Ops:
  0.0 63.9 %shard_map.64 = f32[64,64,256]{2,1,0:T(8,128)} custom-call(f32[8]{0:T(128)} %table_ref.1, s32[64,64]{1,0:T(8,128)} %east_ref.1, s32[64,64]{1,0:T(8,128)} %south_ref.1, f32[64,64]{1,0:T(8,128)} %leak_ref.1, s32[64,64]{1,0:T(8,128)} %pad_ref.1, f32[64,64,256]{2,1,0:T(8,128)} %x_ref.1), custom_call_target="tpu_custom_call" | custom-call | tf_op jit(solution)/shard_map/pallas_call | solution.py:284
  63.9 4.7 %copy.8 = f32[64,64,256]{2,1,0:T(8,128)} copy(f32[64,64,256]{2,1,0:T(8,128)} %shard_map.64) | data formatting | bytes 8388608

commit v2 on v1

--- a/solution.py
+++ b/solution.py
@@ -32,6 +32,26 @@
     return field
 
 
+def loop(lo, count, width, compute):
+    def turn(start, size):
+        pending = [compute(start + u) for u in range(size)]
+        for stores in pending:
+            for put in stores:
+                put()
+
+    turns, rest = count // width, count % width
+    if turns:
+        lax.fori_loop(0, turns, lambda t, c: (turn(lo + t * width, width), c)[1], 0)
+    if rest:
+        turn(lo + turns * width, rest)
+
+
+def setter(ref, index, value):
+    def put():
+        ref[index] = value
+    return put
+
+
 def kernel(
     nx, ny, rows, cols,
     table_ref, east_ref, south_ref, leak_ref, pad_ref, x_ref, o_ref,
@@ -47,10 +67,7 @@
     poly = polynomial()
 
     barrier = pltpu.get_barrier_semaphore()
-    peers = [
-        (north, my), (south, my), (mx, west), (mx, east),
-        (north, west), (north, east), (south, west), (south, east),
-    ]
+    peers = [(north, my), (south, my), (mx, west), (mx, east)]
     for peer in peers:
         pl.semaphore_signal(barrier, inc=1, device_id=peer, device_id_type=MESH)
     own = pltpu.make_async_copy(x_ref, load.at[pl.ds(G, rows)], local_sem)
@@ -100,22 +117,21 @@
     to_left, to_right = pl.ds(0, G), pl.ds(G, G)
     D = G - 1
 
-    def side(start, count, at, row_from, vertical):
+    def side(count, at, ref, row_from):
         return [
             send(
-                x_ref.at[pl.ds(row_from, count), high],
+                ref.at[pl.ds(row_from, count), high],
                 eload.at[0, pl.ds(at, count), to_left],
-                (vertical, east),
+                (mx, east),
             ),
             send(
-                x_ref.at[pl.ds(row_from, count), low],
+                ref.at[pl.ds(row_from, count), low],
                 eload.at[1, pl.ds(at, count), to_right],
-                (vertical, west),
+                (mx, west),
             ),
         ]
 
-    first = side(0, half, G, 0, mx)
-    first += side(0, D, G - D, rows - D, south)
+    first = side(half, G, x_ref, 0)
 
     cf_n.wait_recv()
     cf_s.wait_recv()
@@ -123,8 +139,7 @@
         tw[f, pl.ds(8, cols), :] = jnp.transpose(cf[f])[0:cols, :]
     tw_w = send(tw.at[:, pl.ds(cols, 8)], tw.at[:, pl.ds(0, 8)], (mx, east))
     tw_e = send(tw.at[:, pl.ds(8, 8)], tw.at[:, pl.ds(cols + 8, 8)], (mx, west))
-    second = side(0, rows - half, G + half, half, mx)
-    second += side(0, D, rows + G, 0, north)
+    second = side(rows - half, G + half, x_ref, half)
 
     def coefficients(e, e_west, s, extra):
         s_north = pltpu.roll(s, 1, 1)
@@ -132,12 +147,14 @@
         pads = jnp.where(extra > PAD_GAIN / 2, PAD_GAIN, 0.0)
         return [e * rd, e_west * rd, s * rd, s_north * rd, rd, pads * rd]
 
-    def spread(values, put, lo, count):
-        def one(r):
+    def spread(values, put, lo, count, width):
+        def block(t):
+            r = lo + t * width
             for q, value in enumerate(values):
-                lane = pltpu.roll(value, lax.rem(128 - (r + 8 - G), 128), 1)
-                put(q, r, jnp.broadcast_to(lane[:, 0:1], value.shape))
-        lax.fori_loop(lo, lo + count, lambda r, c: (one(r), c)[1], 0)
+                rolled = pltpu.roll(value, 128 - (r + 8 - G), 1)
+                for u in range(width):
+                    put(q, r + u, jnp.broadcast_to(rolled[:, u : u + 1], value.shape))
+        lax.fori_loop(0, count // width, lambda t, c: (block(t), c)[1], 0)
 
     def put_own(q, r, value):
         bc[q, r] = value
@@ -149,29 +166,25 @@
     e_west = jnp.where(column == 0, e_first, pltpu.roll(e_own, 1, 0))
     spread(
         coefficients(e_own, e_west, tw[1, pl.ds(8, cols), :], tw[2, pl.ds(8, cols), :]),
-        put_own, G, rows,
+        put_own, G, rows, 8,
     )
 
     def source(lo, count):
-        def one(r, c):
-            for h in halves:
-                src[r, :, h] = bc[5, r] - load[r, :, h] * bc[4, r]
-            return c
-        lax.fori_loop(lo, lo + count, one, 0)
+        def one(r):
+            return [
+                setter(src, (r, slice(None), h), bc[5, r] - load[r, :, h] * bc[4, r])
+                for h in halves
+            ]
+        loop(lo, count, 2, one)
 
     chain = [src, v1, v2, v3]
     echain = [esrc, e1, e2, e3]
 
-    def store(k, r, h, value):
-        if k == ITERS:
-            o_ref[r - G, :, h] = value
-        else:
-            chain[k][r, :, h] = value
-
     def step(k, lo, count):
         vin = chain[k - 1]
 
-        def one(r, c):
+        def one(r):
+            stores = []
             for h in halves:
                 row = vin[r, :, h]
                 total = bc[0, r] * pltpu.roll(row, cols - 1, 0)
@@ -180,14 +193,22 @@
                 total += bc[3, r] * vin[r - 1, :, h]
                 if k == 1:
                     total = total * poly[ITERS]
-                store(k, r, h, total + poly[ITERS - k] * src[r, :, h])
-            return c
-
-        lax.fori_loop(lo, lo + count, one, 0)
+                total += poly[ITERS - k] * src[r, :, h]
+                out, at = (o_ref, r - G) if k == ITERS else (chain[k], r)
+                stores.append(setter(out, (at, slice(None), h), total))
+            return stores
+
+        loop(lo, count, 2, one)
 
     own.wait()
     source(G, rows)
-    for k in range(1, ITERS + 1):
+    step(1, G + 1, rows - 2)
+
+    ld_n.wait_recv()
+    ld_s.wait_recv()
+    first += side(D, G - D, load, G - D)
+    second += side(D, rows + G, load, rows + G)
+    for k in range(2, ITERS + 1):
         step(k, G + k, rows - 2 * k)
 
     tw_w.wait_recv()
@@ -200,17 +221,15 @@
         )
 
     k_own = wide(8, cols)
-    spread(k_own, put_own, 0, G)
-    spread(k_own, put_own, rows + G, G)
+    spread(k_own, put_own, 0, G, G)
+    spread(k_own, put_own, rows + G, G, G)
     k_left, k_right = wide(8 - G, 2 * G), wide(8 + cols - G, 2 * G)
 
     def put_edge(w, q, r, value):
         ebc[w, q, r] = value
 
-    spread(k_left, functools.partial(put_edge, 0), 0, rows + 2 * G)
-    spread(k_right, functools.partial(put_edge, 1), 0, rows + 2 * G)
-    ld_n.wait_recv()
-    ld_s.wait_recv()
+    spread(k_left, functools.partial(put_edge, 0), 0, rows + 2 * G, 8)
+    spread(k_right, functools.partial(put_edge, 1), 0, rows + 2 * G, 8)
     source(0, G)
     source(rows + G, G)
     for k in range(1, ITERS + 1):
@@ -221,20 +240,22 @@
     tiles = [pl.ds(0, 2 * G), pl.ds(cols - 2 * G, 2 * G)]
 
     def edge_source(lo, count):
-        def one(r, c):
+        def one(r):
+            stores = []
             for h in halves:
                 for w in range(2):
                     ghost = ebc[w, 5, r] - eload[w, r, :, h] * ebc[w, 4, r]
                     mine = pltpu.roll(src[r, tiles[w], h], G, 0)
                     keep = lane_row < G if w == 0 else lane_row >= G
-                    esrc[w, r, :, h] = jnp.where(keep, ghost, mine)
-            return c
-        lax.fori_loop(lo, lo + count, one, 0)
+                    stores.append(setter(esrc, (w, r, slice(None), h), jnp.where(keep, ghost, mine)))
+            return stores
+        loop(lo, count, 4, one)
 
     def edge_step(k, lo, count):
         vin, base = echain[k - 1], chain[k - 1]
 
-        def one(r, c):
+        def one(r):
+            stores = []
             for h in halves:
                 for w in range(2):
                     row = vin[w, r, :, h]
@@ -251,14 +272,14 @@
                         total = total * poly[ITERS]
                     total += poly[ITERS - k] * esrc[w, r, :, h]
                     if k < ITERS:
-                        echain[k][w, r, :, h] = total
+                        stores.append(setter(echain[k], (w, r, slice(None), h), total))
                     else:
                         keep = lane_row < G if w == 0 else lane_row >= G
                         mixed = jnp.where(keep, pltpu.roll(total, G, 0), o_ref[r - G, tiles[w], h])
-                        o_ref[r - G, tiles[w], h] = mixed
-            return c
-
-        lax.fori_loop(lo, lo + count, one, 0)
+                        stores.append(setter(o_ref, (r - G, tiles[w], h), mixed))
+            return stores
+
+        loop(lo, count, 4, one)
 
     for copy in first:
         copy.wait_recv()
@@ -283,7 +304,7 @@
     copies = 7 + 8
     return pl.pallas_call(
         functools.partial(kernel, nx, ny, rows, cols),
-        out_shape=jax.ShapeDtypeStruct(load_current.shape, f32),
+        out_shape=pltpu.VMEM(load_current.shape, f32),
         in_specs=[pl.BlockSpec(memory_space=pltpu.SMEM), vmem, vmem, vmem, vmem,
                   pl.BlockSpec(memory_space=pl.ANY)],
         out_specs=vmem,
@@ -309,7 +330,7 @@
             pltpu.SemaphoreType.DMA((copies,)),
         ],
         compiler_params=pltpu.CompilerParams(
-            collective_id=0, has_side_effects=True, vmem_limit_bytes=67043328,
+            collective_id=0, has_side_effects=True, vmem_limit_bytes=57 * 2**20,
         ),
     )(cond_table, east_class, south_class, leakage, pad_mask, load_current)
 

time: 68.8 us -> 39.3 us (0.57)
  Pallas kernels: 63.9 us -> 37.1 us
  local copies, waits for them, and re-layouts: 4.7 us -> 2.02 us
    pallas_call x1, Pallas kernels: 63.9 us -> 37.1 us  [body(): pl.pallas_call(functools.partial(kernel, nx, ny, rows, cols), out_shape=p...]
    unnamed x1, local copies, waits for them, and re-layouts: 4.7 us -> 2.02 us
where the time goes in v2:
time: 39.3 us; the launch traced here: 39.1 us
  Pallas kernels  37.1 us (94%)
  local copies, waits for them, and re-layouts  2.02 us (5%)
    pallas_call x1, Pallas kernels, body(): pl.pallas_call(functools.partial(kernel, nx, ny, rows, cols), out_shape=p...  37.1 us
    unnamed x1, local copies, waits for them, and re-layouts  2.02 us

profile of v2, /device:TPU:0, one launch (start us, length us, event | category | flops | bytes accessed | tf_op | source)
XLA Modules:
  0.0 39.1 jit_solution(9878287378692791328)
XLA Ops:
  0.0 37.1 %shard_map.64 = f32[64,64,256]{2,1,0:T(8,128)S(1)} custom-call(f32[8]{0:T(128)} %table_ref.1, s32[64,64]{1,0:T(8,128)} %east_ref.1, s32[64,64]{1,0:T(8,128)} %south_ref.1, f32[64,64]{1,0:T(8,128)} %leak_ref.1, s32[64,64]{1,0:T(8,128)} %pad_ref.1, f32[64,64,256]{2,1,0:T(8,128)} %x_ref.1), custom_call_target="tpu_custom_call" | custom-call | tf_op jit(solution)/shard_map/pallas_call | solution.py:305
  37.1 2.0 %copy.8 = f32[64,64,256]{2,1,0:T(8,128)} copy(f32[64,64,256]{2,1,0:T(8,128)S(1)} %shard_map.64) | data formatting | bytes 8388608

commit v3 on v2

v3 whole, which is shorter than its diff:
```python
import functools

import jax
import jax.numpy as jnp
from jax import lax
from jax.experimental import pallas as pl
from jax.experimental.pallas import tpu as pltpu
from jax.sharding import PartitionSpec as P

ITERS = 4
PAD_GAIN = 8.0
SPECTRAL_BOUND = 0.995
G = ITERS
MESH = pl.DeviceIdType.MESH
CHUNKS = 2


def polynomial():
    weights = [1.0]
    for k in range(1, ITERS):
        if k == 1:
            weights.append(1.0 / (1.0 - SPECTRAL_BOUND**2 / 2.0))
        else:
            weights.append(1.0 / (1.0 - SPECTRAL_BOUND**2 * weights[-1] / 4.0))
    size = ITERS + 1
    previous = [1.0] + [0.0] * (size - 1)
    field = [1.0, 1.0] + [0.0] * (size - 2)
    for k in range(1, ITERS):
        jac = [1.0] + field[:-1]
        updated = [weights[k] * (a - b) + b for a, b in zip(jac, previous)]
        previous, field = field, updated
    return field


def loop(lo, count, width, compute):
    def turn(start, size):
        pending = [compute(start + u) for u in range(size)]
        for stores in pending:
            for put in stores:
                put()

    turns, rest = count // width, count % width
    if turns:
        lax.fori_loop(0, turns, lambda t, c: (turn(lo + t * width, width), c)[1], 0)
    if rest:
        turn(lo + turns * width, rest)


def setter(ref, index, value):
    def put():
        ref[index] = value
    return put


def kernel(
    nx, ny, rows, cols,
    table_ref, east_ref, south_ref, leak_ref, pad_ref, x_ref, o_ref,
    cf, tw, load, src, v1, v2, v3, bc,
    eload, west_bc, east_bc,
    local_sem, send_sem, recv_sem,
):
    mx, my = lax.axis_index("gx"), lax.axis_index("gy")
    north, south = lax.rem(mx + nx - 1, nx), lax.rem(mx + 1, nx)
    west, east = lax.rem(my + ny - 1, ny), lax.rem(my + 1, ny)
    cases = x_ref.shape[2]
    halves = [slice(h * 128, (h + 1) * 128) for h in range(cases // 128)]
    poly = polynomial()

    barrier = pltpu.get_barrier_semaphore()
    peers = [(north, my), (south, my), (mx, west), (mx, east)]
    for peer in peers:
        pl.semaphore_signal(barrier, inc=1, device_id=peer, device_id_type=MESH)
    own = pltpu.make_async_copy(x_ref, load.at[pl.ds(G, rows)], local_sem)
    own.start()

    def lookup(classes):
        value = jnp.full(classes.shape, table_ref[0], jnp.float32)
        for c in range(1, table_ref.shape[0]):
            value = jnp.where(classes == c, table_ref[c], value)
        return value

    blank = jnp.zeros((rows, 128 - cols), jnp.float32)
    fields = [
        lookup(east_ref[...]),
        lookup(south_ref[...]),
        leak_ref[...] + PAD_GAIN * pad_ref[...].astype(jnp.float32),
    ]
    for f in range(3):
        cf[f, pl.ds(8, rows), :] = jnp.concatenate([fields[f], blank], axis=1)
    above, below = jnp.zeros((8, 128), jnp.float32), jnp.zeros((120 - rows, 128), jnp.float32)
    for f in range(3):
        square = jnp.concatenate([above, jnp.concatenate([fields[f], blank], axis=1), below], axis=0)
        tw[f, pl.ds(8, cols), :] = jnp.transpose(square)[0:cols, :]

    pl.semaphore_wait(barrier, len(peers))

    counter = [0]

    def send(source, target, device):
        n = counter[0]
        counter[0] += 1
        copy = pltpu.make_async_remote_copy(
            src_ref=source, dst_ref=target,
            send_sem=send_sem.at[n], recv_sem=recv_sem.at[n],
            device_id=device, device_id_type=MESH,
        )
        copy.start()
        return copy

    cf_n = send(cf.at[:, pl.ds(rows, 8)], cf.at[:, pl.ds(0, 8)], (south, my))
    cf_s = send(cf.at[:, pl.ds(8, 8)], cf.at[:, pl.ds(rows + 8, 8)], (north, my))
    ld_n = send(x_ref.at[pl.ds(rows - G, G)], load.at[pl.ds(0, G)], (south, my))
    ld_s = send(x_ref.at[pl.ds(0, G)], load.at[pl.ds(rows + G, G)], (north, my))
    half = rows // CHUNKS
    low, high = pl.ds(0, G), pl.ds(cols - G, G)
    to_left, to_right = pl.ds(0, G), pl.ds(G, G)
    D = G - 1

    def side(count, at, ref, row_from):
        return [
            send(
                ref.at[pl.ds(row_from, count), high],
                eload.at[0, pl.ds(at, count), to_left],
                (mx, east),
            ),
            send(
                ref.at[pl.ds(row_from, count), low],
                eload.at[1, pl.ds(at, count), to_right],
                (mx, west),
            ),
        ]

    first = side(half, G, x_ref, 0)

    def ratios(e, e_west, s, s_north, extra):
        rd = 1.0 / (e + e_west + s + s_north + extra)
        pads = jnp.where(extra > PAD_GAIN / 2, PAD_GAIN, 0.0)
        return [e * rd, e_west * rd, s * rd, s_north * rd, rd, pads * rd]

    def spread(e, s, extra, before, put, lo, count, width):
        size = e.shape[0]
        first = lax.broadcasted_iota(jnp.int32, (size, 128), 0) == 0

        def block(t):
            r = lo + t * width
            amount = 128 - (r + 8 - G)
            e_at, s_at, x_at = (pltpu.roll(value, amount, 1) for value in (e, s, extra))
            w_at = pltpu.roll(before, amount, 1)
            over = lambda value, u: jnp.broadcast_to(value[:, u : u + 1], (value.shape[0], 128))
            s_north = over(s_at, 127)
            for u in range(width):
                e_now, s_now = over(e_at, u), over(s_at, u)
                head = jnp.broadcast_to(over(w_at, u)[7:8, :], (size, 128))
                e_west = jnp.where(first, head, pltpu.roll(e_now, 1, 0))
                for q, value in enumerate(ratios(e_now, e_west, s_now, s_north, over(x_at, u))):
                    put(q, r + u, value)
                s_north = s_now
        lax.fori_loop(0, count // width, lambda t, c: (block(t), c)[1], 0)

    def put_own(q, r, value):
        bc[q, r] = value

    area = pl.ds(8, cols)
    own_fields = [tw[f, area, :] for f in range(3)]
    spread(*own_fields, tw[0, area, :][0:8], put_own, G, rows, 8)

    cf_n.wait_recv()
    cf_s.wait_recv()
    for f in range(3):
        tw[f, pl.ds(8, cols), :] = jnp.transpose(cf[f])[0:cols, :]
    tw_w = send(tw.at[:, pl.ds(cols, 8)], tw.at[:, pl.ds(0, 8)], (mx, east))
    tw_e = send(tw.at[:, pl.ds(8, 8)], tw.at[:, pl.ds(cols + 8, 8)], (mx, west))
    second = side(rows - half, G + half, x_ref, half)

    chain = [src, v1, v2, v3]

    def source(lo, count):
        def one(r):
            return [
                setter(src, (r, n, pl.ds(8, cols)), bc[5, r] - load[r, :, h] * bc[4, r])
                for n, h in enumerate(halves)
            ]
        loop(lo, count, 2, one)

    def update(k, r, n, at, size, coefs):
        vin = chain[k - 1]
        total = coefs[0] * vin[r, n, pl.ds(at + 1, size)]
        total += coefs[1] * vin[r, n, pl.ds(at - 1, size)]
        total += coefs[2] * vin[r + 1, n, pl.ds(at, size)]
        total += coefs[3] * vin[r - 1, n, pl.ds(at, size)]
        if k == 1:
            total = total * poly[ITERS]
        return total + poly[ITERS - k] * src[r, n, pl.ds(at, size)]

    def step(k, lo, count):
        def one(r):
            stores = []
            coefs = [bc[q, r] for q in range(4)]
            for n, h in enumerate(halves):
                total = update(k, r, n, 8, cols, coefs)
                if k == ITERS:
                    stores.append(setter(o_ref, (r - G, slice(None), h), total))
                else:
                    stores.append(setter(chain[k], (r, n, pl.ds(8, cols)), total))
            return stores

        loop(lo, count, 2, one)

    own.wait()
    source(G, rows)
    step(1, G + 2, rows - 3)

    ld_n.wait_recv()
    ld_s.wait_recv()
    first += side(D, G - D, load, G - D)
    second += side(D, rows + G, load, rows + G)
    for k in range(2, ITERS + 1):
        step(k, G + k + 1, rows - 2 * k - 1)

    tw_w.wait_recv()
    tw_e.wait_recv()

    def put_edge(w, q, r, value):
        (west_bc, east_bc)[w][q, r] = value

    def wide(start, size, *rest):
        fields = [tw[f, pl.ds(start, size), :] for f in range(3)]
        row = tw[0, pl.ds(max(start - 1, 0), 1), :]
        spread(*fields, jnp.broadcast_to(row, (8, 128)), *rest)

    wide(8, cols, put_own, 0, G + 1, G + 1)
    wide(8, cols, put_own, rows + G, G, G)
    wide(0, 16, functools.partial(put_edge, 0), 0, rows + 2 * G, 8)
    wide(8 + cols - G, 2 * G, functools.partial(put_edge, 1), 0, rows + 2 * G, 8)
    source(0, G + 1)
    source(rows + G, G)
    for k in range(1, ITERS + 1):
        step(k, k, G + 1)
        step(k, rows + 2 * G - k - G, G)

    lane_row = lax.broadcasted_iota(jnp.int32, (2 * G, 128), 0)
    starts = [9 - G, 8 + cols - G]
    tiles = [pl.ds(start, 2 * G) for start in starts]
    ghosts = [pl.ds(8 - G, 2 * G), tiles[1]]
    mine = [pl.ds(0, G + 1), pl.ds(cols - G, G)]
    inner = [slice(G - 1, 2 * G), slice(0, G)]
    west_at = [pl.ds(9 - G, 2 * G)] * 4 + [pl.ds(8 - G, 2 * G)] * 2

    def edge_coef(w, q, r):
        return east_bc[q, r] if w else west_bc[q, r, west_at[q]]

    def edge_source(lo, count):
        def one(r):
            stores = []
            for n, h in enumerate(halves):
                near = pltpu.roll(load[r, pl.ds(0, 2 * G), h], G, 0)
                far = pltpu.roll(load[r, pl.ds(cols - 2 * G, 2 * G), h], G, 0)
                for w in range(2):
                    ghost = lane_row < G if w == 0 else lane_row >= G
                    full = jnp.where(ghost, eload[w, r, :, h], far if w else near)
                    value = edge_coef(w, 5, r) - full * edge_coef(w, 4, r)
                    stores.append(setter(src, (r, n, ghosts[w]), value))
            return stores
        loop(lo, count, 4, one)

    def edge_step(k, lo, count):
        def one(r):
            stores = []
            for w in range(2):
                coefs = [edge_coef(w, q, r) for q in range(4)]
                for n, h in enumerate(halves):
                    total = update(k, r, n, starts[w], 2 * G, coefs)
                    if k < ITERS:
                        stores.append(setter(chain[k], (r, n, tiles[w]), total))
                    else:
                        stores.append(setter(o_ref, (r - G, mine[w], h), total[inner[w]]))
            return stores

        loop(lo, count, 4, one)

    for copy in first:
        copy.wait_recv()
    cut = G + half
    edge_source(0, cut)
    for k in range(1, ITERS + 1):
        edge_step(k, k, cut - 2 * k)
    for copy in second:
        copy.wait_recv()
    edge_source(cut, rows + 2 * G - cut)
    for k in range(1, ITERS + 1):
        edge_step(k, cut - k, rows + 2 * G - cut)
    for copy in [cf_n, cf_s, ld_n, ld_s, tw_w, tw_e] + first + second:
        copy.wait_send()


def body(nx, ny, east_class, south_class, cond_table, leakage, pad_mask, load_current):
    rows, cols, cases = load_current.shape
    tall = rows + 2 * G
    f32 = jnp.float32
    vmem = pl.BlockSpec(memory_space=pltpu.VMEM)
    copies = 6 + 8
    return pl.pallas_call(
        functools.partial(kernel, nx, ny, rows, cols),
        out_shape=pltpu.VMEM(load_current.shape, f32),
        in_specs=[pl.BlockSpec(memory_space=pltpu.SMEM), vmem, vmem, vmem, vmem,
                  pl.BlockSpec(memory_space=pl.ANY)],
        out_specs=vmem,
        scratch_shapes=[
            pltpu.VMEM((3, 128, 128), f32),
            pltpu.VMEM((3, cols + 16, 128), f32),
            pltpu.VMEM((tall, cols, cases), f32),
            pltpu.VMEM((tall, cases // 128, cols + 16, 128), f32),
            pltpu.VMEM((tall, cases // 128, cols + 16, 128), f32),
            pltpu.VMEM((tall, cases // 128, cols + 16, 128), f32),
            pltpu.VMEM((tall, cases // 128, cols + 16, 128), f32),
            pltpu.VMEM((6, tall, cols, 128), f32),
            pltpu.VMEM((2, tall, 2 * G, cases), f32),
            pltpu.VMEM((6, tall, 16, 128), f32),
            pltpu.VMEM((6, tall, 2 * G, 128), f32),
            pltpu.SemaphoreType.DMA,
            pltpu.SemaphoreType.DMA((copies,)),
            pltpu.SemaphoreType.DMA((copies,)),
        ],
        compiler_params=pltpu.CompilerParams(
            collective_id=0, has_side_effects=True, vmem_limit_bytes=57 * 2**20,
        ),
    )(cond_table, east_class, south_class, leakage, pad_mask, load_current)


def solution(mesh):
    in_specs = (
        P("gx", "gy"),
        P("gx", "gy"),
        P(),
        P("gx", "gy"),
        P("gx", "gy"),
        P("gx", "gy", None),
    )
    out_specs = P("gx", "gy", None)
    call = functools.partial(body, mesh.shape["gx"], mesh.shape["gy"])
    return jax.shard_map(call, mesh=mesh, in_specs=in_specs, out_specs=out_specs, check_vma=False)
```

time: 39.3 us -> 28.6 us (0.73)
  Pallas kernels: 37.1 us -> 26.4 us
    pallas_call x1, Pallas kernels: 37.1 us -> 26.4 us  [body(): pl.pallas_call(functools.partial(kernel, nx, ny, rows, cols), out_shape=p...]
where the time goes in v3:
time: 28.6 us; the launch traced here: 28.5 us
  Pallas kernels  26.4 us (92%)
  local copies, waits for them, and re-layouts  2.02 us (7%)
    pallas_call x1, Pallas kernels, body(): pl.pallas_call(functools.partial(kernel, nx, ny, rows, cols), out_shape=p...  26.4 us
    unnamed x1, local copies, waits for them, and re-layouts  2.02 us

profile of v3, /device:TPU:0, one launch (start us, length us, event | category | flops | bytes accessed | tf_op | source)
XLA Modules:
  0.0 28.5 jit_solution(9079638634316638878)
XLA Ops:
  0.0 26.4 %shard_map.64 = f32[64,64,256]{2,1,0:T(8,128)S(1)} custom-call(f32[8]{0:T(128)} %table_ref.1, s32[64,64]{1,0:T(8,128)} %east_ref.1, s32[64,64]{1,0:T(8,128)} %south_ref.1, f32[64,64]{1,0:T(8,128)} %leak_ref.1, s32[64,64]{1,0:T(8,128)} %pad_ref.1, f32[64,64,256]{2,1,0:T(8,128)} %x_ref.1), custom_call_target="tpu_custom_call" | custom-call | tf_op jit(solution)/shard_map/pallas_call | solution.py:302
  26.4 2.0 %copy.8 = f32[64,64,256]{2,1,0:T(8,128)} copy(f32[64,64,256]{2,1,0:T(8,128)S(1)} %shard_map.64) | data formatting | bytes 8388608
